TPU v7x, 32 devices: a whole 2x2x4 slice. The times are simulated.
32 devices in a mesh: samp: 16 (over z, y, core), snp: 2 (over x).
Axes of the slice: x: 2, y: 2, z: 4, core: 2. Of those that a mesh axis runs over, the one named last changes fastest.
Arguments:
- genotype: int32 [16384, 4096], P('samp', 'snp'), may hold values from 0 to 3, as said below
- basis: bfloat16 [4096, 40], P('snp'), may hold values from -6 to 6
Outputs:
- sample_scores: bfloat16 [16384, 40], P('samp')
- snp_block: float32 [4096, 40], P('snp')
Inputs may be any that keep to these rules, and one draw needn't show every extreme that they name: `genotype`: the value 3 marks a missing call; 0, 1 and 2 are dosages.
All inputs are finite; a program needn't handle non-finite values.
Results may differ from a plain program's by a relative error of at most 0.0065.
Values may be sent and summed in bfloat16 or wider, within the bound.
A program may use at most 64 MiB of HBM per device.

v0:
```python
import jax
import jax.numpy as jnp
from jax import lax
from jax.sharding import PartitionSpec as P

ITERS = 2


def per_device(genotype, basis):
    observed = genotype < 3
    dosage = jnp.where(observed, genotype, 0).astype(jnp.float32)
    allele_sum, called = lax.psum(
        (jnp.sum(dosage, axis=0), jnp.sum(observed.astype(jnp.float32), axis=0)), "samp"
    )
    freq = (allele_sum + 1.0) / (2.0 * called + 2.0)
    scale = 1.0 / jnp.sqrt(2.0 * freq * (1.0 - freq))
    standard = jnp.where(observed, (dosage - 2.0 * freq) * scale, 0.0).astype(jnp.bfloat16)
    row_count = genotype.shape[0]
    total = row_count * lax.axis_size("samp")
    contract = (((0,), (0,)), ((), ()))
    block = basis
    for step in range(ITERS):
        scores = lax.psum(jnp.dot(standard, block, preferred_element_type=jnp.float32), "snp")
        sample_scores = scores.astype(jnp.bfloat16)
        local = lax.dot_general(
            standard, sample_scores, contract, preferred_element_type=jnp.float32
        )
        snp_block = lax.psum(local, "samp") / total
        block = snp_block.astype(jnp.bfloat16)
    return (sample_scores, snp_block)


def solution(mesh):
    placed = (P("samp", "snp"), P("snp", None))
    return jax.shard_map(
        per_device,
        mesh=mesh,
        in_specs=placed,
        out_specs=(P("samp", None), P("snp", None)),
        check_vma=False,
    )
```

profile of v0, /device:TPU:8, one launch (start us, length us, event | category | flops | bytes accessed | tf_op | source)
XLA Modules:
  0.0 305.8 jit_solution(3003615969748180968)
XLA Ops:
  7.2 0.0 copy-start
  7.2 0.0 all-reduce.6.cloned.1.call-start
  7.2 5.1 %convert_reduce_fusion.1 = (f32[2048]{0:T(1024)S(1)}, f32[2048]{0:T(1024)S(1)}) fusion(s32[1024,2048]{1,0:T(8,128)} %param.2), kind=kLoop, calls=%fused_computation.2 | loop fusion | flops 12578816 | bytes 8404992 | tf_op jit(solution)/shard_map/reduce_sum | solution.py:13
  12.3 53.5 %all-reduce = (f32[2048]{0:T(1024)S(1)}, f32[2048]{0:T(1024)S(1)}) all-reduce(f32[2048]{0:T(1024)S(1)} %get-tuple-element.3, f32[2048]{0:T(1024)S(1)} %get-tuple-element.2), channel_id=1, replica_groups=mesh['samp'=16,'snp'=2] {'samp'}, use_global_device_ids=true, to_apply=%region_3.4 | all-reduce | flops 4096 | bytes 32768 | tf_op jit(solution)/shard_map/psum | solution.py:12
  65.8 4.4 %select_convert_fusion = bf16[1024,2048]{1,0:T(8,128)(2,1)S(1)} fusion(s32[1024,2048]{1,0:T(8,128)} %param.2, f32[2048]{0:T(1024)S(1)} %get-tuple-element.7, f32[2048]{0:T(1024)S(1)} %get-tuple-element.6), kind=kLoop, calls=%fused_computation | loop fusion | flops 14680064 | bytes 12599296 | tf_op jit(solution)/shard_map/convert_element_type | solution.py:17
  70.2 0.0 copy-start.1
  70.2 1.9 copy-done.1
  72.1 0.0 copy-done
  72.1 1.2 fusion.5
  73.4 15.7 %all-reduce.9 = bf16[1024,40]{1,0:T(8,128)(2,1)S(1)} all-reduce(f32[1024,40]{1,0:T(8,128)S(1)} %fusion.5), channel_id=1, replica_groups=mesh['samp'=16,'snp'=2] {'snp'}, use_global_device_ids=true, to_apply=%region_4.5 | all-reduce | flops 40960 | bytes 245760 | tf_op jit(solution)/shard_map/psum | solution.py:23
  89.0 3.8 %fusion.7 = f32[2048,40]{0,1:T(8,128)} fusion(bf16[1024,2048]{1,0:T(8,128)(2,1)} %copy-done.1, bf16[1024,40]{1,0:T(8,128)(2,1)S(1)} %all-reduce.9), kind=kOutput, calls=%fused_computation.16 | convolution fusion | flops 167772160 | bytes 4603904 | tf_op jit(solution)/shard_map/dot_general | solution.py:25
  92.8 0.0 all-reduce.6.cloned.1.call-update
  92.8 0.0 all-reduce.8.cloned.1.call-start
  92.9 96.7 %all-reduce.6.cloned.1.call-done = f32[2048,40]{0,1:T(8,128)} async-done(((f32[2048,40]{0,1:T(8,128)}), f32[2048,40]{0,1:T(8,128)}) %all-reduce.6.cloned.1.call-update) | async-done | bytes 327696 | tf_op jit(solution)/shard_map/psum | solution.py:28
  189.6 3.6 %fusion.2 = f32[1024,40]{0,1:T(8,128)S(1)} fusion(bf16[1024,2048]{1,0:T(8,128)(2,1)} %copy-done.1, f32[2048,40]{0,1:T(8,128)} %all-reduce.6.cloned.1.call-done), kind=kOutput, calls=%fused_computation.7 | convolution fusion | flops 167936000 | bytes 4685824 | tf_op jit(solution)/shard_map/dot_general | solution.py:23
  193.2 10.0 %all-reduce.10 = bf16[1024,40]{0,1:T(8,128)(2,1)S(1)} all-reduce(f32[1024,40]{0,1:T(8,128)S(1)} %fusion.2), channel_id=1, replica_groups=mesh['samp'=16,'snp'=2] {'snp'}, use_global_device_ids=true, to_apply=%region_6.7 | all-reduce | flops 40960 | bytes 245760 | tf_op jit(solution)/shard_map/psum | solution.py:23
  203.2 0.0 copy-start.2
  203.2 3.8 %fusion.6 = f32[2048,40]{0,1:T(8,128)} fusion(bf16[1024,2048]{1,0:T(8,128)(2,1)} %copy-done.1, bf16[1024,40]{0,1:T(8,128)(2,1)S(1)} %all-reduce.10), kind=kOutput, calls=%fused_computation.15 | convolution fusion | flops 167772160 | bytes 4603904 | tf_op jit(solution)/shard_map/dot_general | solution.py:25
  206.9 0.0 all-reduce.8.cloned.1.call-update
  207.0 90.2 %all-reduce.8.cloned.1.call-done = f32[2048,40]{0,1:T(8,128)} async-done(((f32[2048,40]{0,1:T(8,128)}), f32[2048,40]{0,1:T(8,128)}) %all-reduce.8.cloned.1.call-update) | async-done | bytes 327696 | tf_op jit(solution)/shard_map/psum | solution.py:28
  297.2 1.7 broadcast_multiply_fusion
  298.9 0.0 copy-done.2
  (1 shorter events, 0.0 us)
Async XLA Ops:
  7.2 65.0 %copy-start = (bf16[2048,40]{0,1:T(8,128)(2,1)S(1)}, bf16[2048,40]{0,1:T(8,128)(2,1)}, u32[]{:S(2)}) copy-start(bf16[2048,40]{0,1:T(8,128)(2,1)} %param.3) | copy-start | bytes 491524
  7.2 182.4 %all-reduce.6.cloned.1.call-start = ((), (), s32[]{:S(2)}) async-start(), calls=%async_computation | async-start | bytes 655360 | tf_op jit(solution)/shard_map/psum | solution.py:28
  70.2 1.9 copy-start.1
  92.8 204.4 %all-reduce.8.cloned.1.call-start = ((), (), s32[]{:S(2)}) async-start(), calls=%async_computation.1 | async-start | bytes 655360 | tf_op jit(solution)/shard_map/psum | solution.py:28
  203.2 95.8 %copy-start.2 = (bf16[1024,40]{0,1:T(8,128)(2,1)}, bf16[1024,40]{0,1:T(8,128)(2,1)S(1)}, u32[]{:S(2)}) copy-start(bf16[1024,40]{0,1:T(8,128)(2,1)S(1)} %all-reduce.10) | copy-start | bytes 245764
Sparse Core Ops, SparseCore 0:
  92.9 96.6 all-reduce.5
  207.1 90.0 all-reduce.7
where the time goes:
time: 306 us
  waiting for transfers between devices  187 us (61%)
  blocking collectives  79.1 us (26%)
  between operations  14.1 us (5%)
  matrix products  12.3 us (4%)
  other arithmetic  11.2 us (4%)
    psum x2, waiting for transfers between devices, per_device(): snp_block = lax.psum(local, 'samp') / total  187 us
    psum x1, blocking collectives, per_device(): lax.psum((jnp.sum(dosage, axis=0), jnp.sum(observed.astype(jnp.float32),...  53.5 us
    psum x2, blocking collectives, per_device(): lax.psum(jnp.dot(standard, block, preferred_element_type=jnp.float32), 's...  25.6 us
    dot_general x2, matrix products, per_device(): lax.dot_general(standard, sample_scores, contract, preferred_element_type...  7.52 us
  transfers between devices with their start and end apart: 2, of which 2 were waited for; matrix products, arithmetic and copies ran while one was open for 0% of the time, Pallas kernels for 0%

commit v1 on v0

--- a/solution.py
+++ b/solution.py
@@ -25,7 +25,7 @@
         local = lax.dot_general(
             standard, sample_scores, contract, preferred_element_type=jnp.float32
         )
-        snp_block = lax.psum(local, "samp") / total
+        snp_block = jnp.sum(lax.all_gather(local, "samp"), axis=0) / total
         block = snp_block.astype(jnp.bfloat16)
     return (sample_scores, snp_block)
 

time: 306 us -> 247 us (0.81)
  waiting for transfers between devices: 187 us -> 115 us
  local copies, waits for them, and re-layouts: 1.93 us -> 14.2 us
    psum x2 -> x0, waiting for transfers between devices: 187 us -> none  [per_device(): snp_block = lax.psum(local, 'samp') / total]
    all_gather x0 -> x2, waiting for transfers between devices: none -> 115 us  [per_device(): snp_block = jnp.sum(lax.all_gather(local, 'samp'), axis=0) / total]
    unnamed x6 -> x10, local copies, waits for them, and re-layouts: 1.93 us -> 14.2 us
where the time goes in v1:
time: 247 us; the launch traced here: 245 us
  waiting for transfers between devices  115 us (47%)
  blocking collectives  79.5 us (32%)
  local copies, waits for them, and re-layouts  14.2 us (6%)
  between operations  14.1 us (6%)
  other arithmetic  12.1 us (5%)
  matrix products  10.1 us (4%)
    all_gather x2, waiting for transfers between devices, per_device(): snp_block = jnp.sum(lax.all_gather(local, 'samp'), axis=0) / total  115 us
    psum x1, blocking collectives, per_device(): lax.psum((jnp.sum(dosage, axis=0), jnp.sum(observed.astype(jnp.float32),...  53.5 us
    psum x2, blocking collectives, per_device(): lax.psum(jnp.dot(standard, block, preferred_element_type=jnp.float32), 's...  26 us
    unnamed x10, local copies, waits for them, and re-layouts  14.2 us
    dot_general x2, matrix products, per_device(): lax.dot_general(standard, sample_scores, contract, preferred_element_type...  7.52 us
    reduce_sum x1, other arithmetic, per_device(): jnp.sum(dosage, axis=0)  5.06 us
  transfers between devices with their start and end apart: 2, of which 2 were waited for; matrix products, arithmetic and copies ran while one was open for 0% of the time, Pallas kernels for 0%

profile of v1, /device:TPU:8, one launch (start us, length us, event | category | flops | bytes accessed | tf_op | source)
XLA Modules:
  0.0 244.8 jit_solution(1473212002994971361)
XLA Ops:
  7.2 0.0 copy-start
  7.2 0.0 all-gather.5.cloned.1.call-start
  7.2 5.1 %convert_reduce_fusion.1 = (f32[2048]{0:T(1024)S(1)}, f32[2048]{0:T(1024)S(1)}) fusion(s32[1024,2048]{1,0:T(8,128)} %param.2), kind=kLoop, calls=%fused_computation.2 | loop fusion | flops 12578816 | bytes 8404992 | tf_op jit(solution)/shard_map/reduce_sum | solution.py:13
  12.3 53.5 %all-reduce = (f32[2048]{0:T(1024)S(1)}, f32[2048]{0:T(1024)S(1)}) all-reduce(f32[2048]{0:T(1024)S(1)} %get-tuple-element.3, f32[2048]{0:T(1024)S(1)} %get-tuple-element.2), channel_id=1, replica_groups=mesh['samp'=16,'snp'=2] {'samp'}, use_global_device_ids=true, to_apply=%region_3.4 | all-reduce | flops 4096 | bytes 32768 | tf_op jit(solution)/shard_map/psum | solution.py:12
  65.8 4.4 %select_convert_fusion = bf16[1024,2048]{1,0:T(8,128)(2,1)S(1)} fusion(s32[1024,2048]{1,0:T(8,128)} %param.2, f32[2048]{0:T(1024)S(1)} %get-tuple-element.7, f32[2048]{0:T(1024)S(1)} %get-tuple-element.6), kind=kLoop, calls=%fused_computation | loop fusion | flops 14680064 | bytes 12599296 | tf_op jit(solution)/shard_map/convert_element_type | solution.py:17
  70.2 2.0 copy-done.1
  72.2 1.2 fusion.5
  73.5 15.7 %all-reduce.3 = bf16[1024,40]{1,0:T(8,128)(2,1)S(1)} all-reduce(f32[1024,40]{1,0:T(8,128)S(1)} %fusion.5), channel_id=1, replica_groups=mesh['samp'=16,'snp'=2] {'snp'}, use_global_device_ids=true, to_apply=%region_4.5 | all-reduce | flops 40960 | bytes 245760 | tf_op jit(solution)/shard_map/psum | solution.py:23
  89.1 3.8 %fusion.7 = f32[2048,40]{0,1:T(8,128)} fusion(bf16[1024,2048]{1,0:T(8,128)(2,1)} %copy-done.1, bf16[1024,40]{1,0:T(8,128)(2,1)S(1)} %all-reduce.3), kind=kOutput, calls=%fused_computation.18 | convolution fusion | flops 167772160 | bytes 4603904 | tf_op jit(solution)/shard_map/dot_general | solution.py:25
  92.9 0.0 all-gather.5.cloned.1.call-update
  92.9 0.0 all-gather.7.cloned.1.call-start
  93.0 61.1 %all-gather.5.cloned.1.call-done = f32[32768,40]{0,1:T(8,128)} async-done(((f32[2048,40]{0,1:T(8,128)}), f32[32768,40]{0,1:T(8,128)}) %all-gather.5.cloned.1.call-update) | async-done | bytes 5242896 | tf_op jit(solution)/shard_map/all_gather | solution.py:28
  154.1 5.5 %copy.4 = f32[5,8,16,2048]{3,2,1,0:T(8,128)S(1)} copy(f32[5,8,16,2048]{3,1,2,0:T(8,128)} %bitcast.17) | data formatting | bytes 10485760
  159.5 0.9 bitcast_reduce_fusion.1
  160.5 1.2 copy-done.2
  161.7 1.4 fusion.2
  163.1 10.3 %all-reduce.4 = bf16[1024,40]{0,1:T(8,128)(2,1)S(1)} all-reduce(f32[1024,40]{0,1:T(8,128)S(1)} %fusion.2), channel_id=1, replica_groups=mesh['samp'=16,'snp'=2] {'snp'}, use_global_device_ids=true, to_apply=%region_6.7 | all-reduce | flops 40960 | bytes 245760 | tf_op jit(solution)/shard_map/psum | solution.py:23
  173.4 0.0 copy-start.3
  173.4 3.8 %fusion.6 = f32[2048,40]{0,1:T(8,128)} fusion(bf16[1024,2048]{1,0:T(8,128)(2,1)} %copy-done.1, bf16[1024,40]{0,1:T(8,128)(2,1)S(1)} %all-reduce.4), kind=kOutput, calls=%fused_computation.17 | convolution fusion | flops 167772160 | bytes 4603904 | tf_op jit(solution)/shard_map/dot_general | solution.py:25
  177.2 0.0 all-gather.7.cloned.1.call-update
  177.2 53.6 %all-gather.7.cloned.1.call-done = f32[32768,40]{0,1:T(8,128)} async-done(((f32[2048,40]{0,1:T(8,128)}), f32[32768,40]{0,1:T(8,128)}) %all-gather.7.cloned.1.call-update) | async-done | bytes 5242896 | tf_op jit(solution)/shard_map/all_gather | solution.py:28
  230.8 5.5 %copy.5 = f32[5,8,16,2048]{3,2,1,0:T(8,128)S(1)} copy(f32[5,8,16,2048]{3,1,2,0:T(8,128)} %bitcast.18) | data formatting | bytes 10485760
  236.3 0.9 bitcast_reduce_fusion
  237.2 0.7 broadcast_multiply_fusion
  (5 shorter events, 0.0 us)
Async XLA Ops:
  7.2 65.1 %copy-start = (bf16[2048,40]{0,1:T(8,128)(2,1)S(1)}, bf16[2048,40]{0,1:T(8,128)(2,1)}, u32[]{:S(2)}) copy-start(bf16[2048,40]{0,1:T(8,128)(2,1)} %param.3) | copy-start | bytes 491524
  7.2 146.9 %all-gather.5.cloned.1.call-start = ((), (), s32[]{:S(2)}) async-start(), calls=%async_computation | async-start | bytes 5570560 | tf_op jit(solution)/shard_map/all_gather | solution.py:28
  70.2 2.0 copy-start.1
  92.9 137.9 %all-gather.7.cloned.1.call-start = ((), (), s32[]{:S(2)}) async-start(), calls=%async_computation.1 | async-start | bytes 5570560 | tf_op jit(solution)/shard_map/all_gather | solution.py:28
  159.5 2.2 copy-start.2
  173.4 62.9 %copy-start.3 = (bf16[1024,40]{0,1:T(8,128)(2,1)}, bf16[1024,40]{0,1:T(8,128)(2,1)S(1)}, u32[]{:S(2)}) copy-start(bf16[1024,40]{0,1:T(8,128)(2,1)S(1)} %all-reduce.4) | copy-start | bytes 245764
Sparse Core Ops, SparseCore 0:
  93.0 60.9 all-gather.4
  177.3 53.4 all-gather.6
